TPU v7x, 32 devices: a whole 2x2x4 slice. The times are simulated.
32 devices in a mesh: wide: 8 (over z, x), narrow: 4 (over y, core).
Axes of the slice: x: 2, y: 2, z: 4, core: 2. Of those that a mesh axis runs over, the one named last changes fastest.
Arguments:
- cost: float32 [1024, 16384], P('wide', 'narrow'), may hold values from 0 to 2
- plan: float32 [1024, 16384], P('wide', 'narrow'), may hold values from 0 to 2
- row_mass: float32 [1024], P('wide'), may hold values from 4096 to 28672
- col_mass: float32 [16384], P('narrow'), may hold values from 256 to 1792
- row_dual: float32 [1024], P('wide'), may hold values from -3 to 3
- col_dual: float32 [16384], P('narrow'), may hold values from -3 to 3
Outputs:
- plan_out: float32 [1024, 16384], P('wide', 'narrow')
- row_out: float32 [1024], P('wide')
- col_out: float32 [16384], P('narrow')
All inputs are finite; a program needn't handle non-finite values.
Results may differ from a plain program's by a relative error of at most 0.0001.
Values sent between devices are 32-bit elements; how exact they have to be, the bound alone decides.
A program may use at most 64 MiB of HBM per device.

v0:
```python
import math
import jax
import jax.numpy as jnp
from jax import lax
from jax.sharding import PartitionSpec as P

ITERS = 4


def shards(cost, plan, row_mass, col_mass, row_dual, col_dual):
    wide_count = lax.axis_size("wide")
    narrow_count = lax.axis_size("narrow")
    total_rows = plan.shape[0] * wide_count
    total_cols = plan.shape[1] * narrow_count
    step_base = 0.9 / math.sqrt(total_rows + total_cols)
    weight = jnp.float32(step_base)
    for step in range(ITERS):
        primal_step = step_base / weight
        dual_step = step_base * weight
        fresh = jnp.maximum(
            plan - primal_step * (cost - row_dual[:, None] - col_dual[None, :]), 0.0
        )
        change = fresh - plan
        extrap = fresh + change
        moved = jnp.sum(change * change)
        row_total = lax.psum(jnp.sum(extrap, axis=1), "narrow")
        new_row = row_dual + dual_step * (row_mass - row_total)
        row_square = jnp.sum((new_row - row_dual) ** 2)
        col_local = jnp.sum(extrap, axis=0)
        col_total = lax.psum(col_local, "wide")
        new_col = col_dual + dual_step * (col_mass - col_total)
        col_share = jnp.sum((new_col - col_dual) ** 2) / wide_count
        dual_share = row_square / narrow_count + col_share
        moved_all = lax.psum(moved, ("wide", "narrow"))
        dual_moved = lax.psum(dual_share, ("wide", "narrow"))
        weight = jnp.sqrt(weight * jnp.sqrt((dual_moved + 1.0) / (moved_all + 1.0)))
        plan, row_dual, col_dual = (fresh, new_row, new_col)
    return (plan, row_dual, col_dual)


def solution(mesh):
    in_specs = (
        P("wide", "narrow"),
        P("wide", "narrow"),
        P("wide"),
        P("narrow"),
        P("wide"),
        P("narrow"),
    )
    out_specs = (P("wide", "narrow"), P("wide"), P("narrow"))
    return jax.shard_map(shards, mesh=mesh, in_specs=in_specs, out_specs=out_specs, check_vma=False)
```

profile of v0, /device:TPU:0, one launch (start us, length us, event | category | flops | bytes accessed | tf_op | source)
XLA Modules:
  0.0 314.4 jit_solution(7714371782723744070)
XLA Ops:
  0.6 0.0 copy-start.1
  0.6 0.0 copy-start.3
  0.7 0.0 copy-start.2
  0.7 0.0 copy-start.4
  0.7 0.0 copy-start
  0.7 4.2 %multiply_reduce_fusion.2 = (f32[]{:T(128)}, f32[4096]{0:T(1024)S(1)}, f32[128]{0:T(128)S(1)}) fusion(f32[128,4096]{1,0:T(8,128)} %param.7, f32[4096]{0:T(1024)} %param.11, f32[128,4096]{1,0:T(8,128)} %param.6, f32[128]{0:T(128)} %param.10), kind=kLoop, calls=%fused_computation.6 | loop fusion | flops 5238655 | bytes 4228100 | tf_op jit(solution)/shard_map/reduce_sum | solution.py:25
  4.9 38.8 %psum.99 = f32[4096]{0:T(1024)S(1)} all-reduce(f32[4096]{0:T(1024)S(1)} %get-tuple-element.12), channel_id=1, replica_groups=mesh['wide'=8,'narrow'=4] {'wide'}, use_global_device_ids=true, to_apply=%region_4.0 | all-reduce | flops 4096 | bytes 32768 | tf_op jit(solution)/shard_map/psum | solution.py:30
  43.7 5.6 %psum.98 = f32[128]{0:T(128)S(1)} all-reduce(f32[128]{0:T(128)S(1)} %get-tuple-element.13), channel_id=1, replica_groups=mesh['wide'=8,'narrow'=4] {'narrow'}, use_global_device_ids=true, to_apply=%region_1.0 | all-reduce | flops 128 | bytes 1024 | tf_op jit(solution)/shard_map/psum | solution.py:26
  49.3 0.0 copy-done.3
  49.3 0.0 copy-done.4
  49.3 0.6 multiply_reduce_fusion.8
  50.6 0.0 copy-done.1
  50.6 0.0 copy-done.2
  50.6 0.6 multiply_reduce_fusion.5
  51.9 37.2 %all-reduce.2 = (f32[]{:T(128)}, f32[]{:T(128)}) all-reduce(f32[]{:T(128)S(6)} %add.94, f32[]{:T(128)} %get-tuple-element.11), channel_id=1, replica_groups=mesh['wide'=8,'narrow'=4] {'wide','narrow'}, use_global_device_ids=true, to_apply=%region_6.0 | all-reduce | flops 2 | bytes 16 | tf_op jit(solution)/shard_map/psum | solution.py:35
  90.5 0.0 copy-done
  90.5 3.7 %multiply_reduce_fusion.1 = (f32[]{:T(128)}, f32[128]{0:T(128)S(1)}, f32[4096]{0:T(1024)S(1)}) fusion(f32[4096]{0:T(1024)S(1)} %get-tuple-element.30, f32[128,4096]{1,0:T(8,128)} %param.6, f32[128]{0:T(128)S(1)} %get-tuple-element.32, f32[]{:T(128)S(6)} %div.39, f32[128,4096]{1,0:T(8,128)S(1)} %copy-done, f32[4096]{0:T(1024)S(1)} %copy-done.1, ...), kind=kLoop, calls=%fused_computation.4 | loop fusion | flops 7860095 | bytes 4245000 | tf_op jit(solution)/shard_map/reduce_sum | solution.py:25
  94.2 6.9 %psum.102 = f32[128]{0:T(128)S(1)} all-reduce(f32[128]{0:T(128)S(1)} %get-tuple-element.9), channel_id=1, replica_groups=mesh['wide'=8,'narrow'=4] {'narrow'}, use_global_device_ids=true, to_apply=%region_10.0 | all-reduce | flops 128 | bytes 1024 | tf_op jit(solution)/shard_map/psum | solution.py:26
  101.1 0.6 multiply_reduce_fusion.7
  102.4 35.6 %psum.103 = f32[4096]{0:T(1024)S(1)} all-reduce(f32[4096]{0:T(1024)S(1)} %get-tuple-element.10), channel_id=1, replica_groups=mesh['wide'=8,'narrow'=4] {'wide'}, use_global_device_ids=true, to_apply=%region_13.0 | all-reduce | flops 4096 | bytes 32768 | tf_op jit(solution)/shard_map/psum | solution.py:30
  138.0 0.6 multiply_reduce_fusion.4
  139.2 37.1 %all-reduce.1 = (f32[]{:T(128)}, f32[]{:T(128)}) all-reduce(f32[]{:T(128)S(6)} %add.100, f32[]{:T(128)} %get-tuple-element.8), channel_id=1, replica_groups=mesh['wide'=8,'narrow'=4] {'wide','narrow'}, use_global_device_ids=true, to_apply=%region_15.0 | all-reduce | flops 2 | bytes 16 | tf_op jit(solution)/shard_map/psum | solution.py:35
  177.8 4.2 %multiply_reduce_fusion = (f32[]{:T(128)}, f32[128]{0:T(128)S(1)}, f32[4096]{0:T(1024)S(1)}) fusion(f32[4096]{0:T(1024)S(1)} %get-tuple-element.26, f32[128,4096]{1,0:T(8,128)} %param.6, f32[128]{0:T(128)S(1)} %get-tuple-element.28, f32[]{:T(128)S(6)} %div.43, f32[4096]{0:T(1024)S(1)} %get-tuple-element.30, f32[128]{0:T(128)S(1)} %get-tuple-element.32, ...), kind=kLoop, calls=%fused_computation.2 | loop fusion | flops 10481535 | bytes 4261900 | tf_op jit(solution)/shard_map/reduce_sum | solution.py:25
  182.0 7.2 %psum.106 = f32[128]{0:T(128)S(1)} all-reduce(f32[128]{0:T(128)S(1)} %get-tuple-element.6), channel_id=1, replica_groups=mesh['wide'=8,'narrow'=4] {'narrow'}, use_global_device_ids=true, to_apply=%region_19.0 | all-reduce | flops 128 | bytes 1024 | tf_op jit(solution)/shard_map/psum | solution.py:26
  189.2 0.6 multiply_reduce_fusion.6
  190.5 35.3 %psum.107 = f32[4096]{0:T(1024)S(1)} all-reduce(f32[4096]{0:T(1024)S(1)} %get-tuple-element.7), channel_id=1, replica_groups=mesh['wide'=8,'narrow'=4] {'wide'}, use_global_device_ids=true, to_apply=%region_22.0 | all-reduce | flops 4096 | bytes 32768 | tf_op jit(solution)/shard_map/psum | solution.py:30
  225.8 0.6 multiply_reduce_fusion.3
  227.0 37.3 %all-reduce = (f32[]{:T(128)}, f32[]{:T(128)}) all-reduce(f32[]{:T(128)S(6)} %add.106, f32[]{:T(128)} %get-tuple-element.5), channel_id=1, replica_groups=mesh['wide'=8,'narrow'=4] {'wide','narrow'}, use_global_device_ids=true, to_apply=%region_24.0 | all-reduce | flops 2 | bytes 16 | tf_op jit(solution)/shard_map/psum | solution.py:35
  265.8 4.9 %fusion.6 = (f32[4096]{0:T(1024)S(1)}, f32[128]{0:T(128)S(1)}, f32[128,4096]{1,0:T(8,128)}) fusion(f32[4096]{0:T(1024)S(1)} %get-tuple-element.26, f32[128,4096]{1,0:T(8,128)} %param.6, f32[128]{0:T(128)S(1)} %get-tuple-element.28, f32[]{:T(128)S(6)} %div.43, f32[4096]{0:T(1024)S(1)} %get-tuple-element.30, f32[128]{0:T(128)S(1)} %get-tuple-element.32, ...), kind=kLoop, calls=%fused_computation.17 | loop fusion | flops 12054400 | bytes 6375948 | tf_op jit(solution)/shard_map/reduce_sum | solution.py:29
  270.7 36.8 %psum.111 = f32[4096]{0:T(1024)S(1)} all-reduce(f32[4096]{0:T(1024)S(1)} %get-tuple-element.3), channel_id=1, replica_groups=mesh['wide'=8,'narrow'=4] {'wide'}, use_global_device_ids=true, to_apply=%region_30.0 | all-reduce | flops 4096 | bytes 32768 | tf_op jit(solution)/shard_map/psum | solution.py:30
  307.5 0.6 multiply_add_fusion
  308.1 5.7 %psum.110 = f32[128]{0:T(128)S(1)} all-reduce(f32[128]{0:T(128)S(1)} %get-tuple-element.4), channel_id=1, replica_groups=mesh['wide'=8,'narrow'=4] {'narrow'}, use_global_device_ids=true, to_apply=%region_28.0 | all-reduce | flops 128 | bytes 1024 | tf_op jit(solution)/shard_map/psum | solution.py:26
  313.9 0.5 multiply_add_fusion.4
Async XLA Ops:
  0.6 49.9 %copy-start.1 = (f32[4096]{0:T(1024)S(1)}, f32[4096]{0:T(1024)}, u32[]{:S(2)}) copy-start(f32[4096]{0:T(1024)} %param.11) | copy-start | bytes 49156
  0.6 48.7 %copy-start.3 = (f32[128]{0:T(128)S(1)}, f32[128]{0:T(128)}, u32[]{:S(2)}) copy-start(f32[128]{0:T(128)} %param.10) | copy-start | bytes 1540
  0.7 49.9 %copy-start.2 = (f32[4096]{0:T(1024)S(1)}, f32[4096]{0:T(1024)}, u32[]{:S(2)}) copy-start(f32[4096]{0:T(1024)} %param.9) | copy-start | bytes 49156
  0.7 48.7 %copy-start.4 = (f32[128]{0:T(128)S(1)}, f32[128]{0:T(128)}, u32[]{:S(2)}) copy-start(f32[128]{0:T(128)} %param.8) | copy-start | bytes 1540
  0.7 89.8 %copy-start = (f32[128,4096]{1,0:T(8,128)S(1)}, f32[128,4096]{1,0:T(8,128)}, u32[]{:S(2)}) copy-start(f32[128,4096]{1,0:T(8,128)} %param.7) | copy-start | bytes 6291460
where the time goes:
time: 315 us; the launch traced here: 314 us
  blocking collectives  284 us (90%)
  other arithmetic  21.7 us (7%)
  between operations  9.03 us (3%)
    psum x4, blocking collectives, shards(): col_total = lax.psum(col_local, 'wide')  147 us
    psum x3, blocking collectives, shards(): dual_moved = lax.psum(dual_share, ('wide', 'narrow'))  112 us
    psum x4, blocking collectives, shards(): row_total = lax.psum(jnp.sum(extrap, axis=1), 'narrow')  25.5 us
    reduce_sum x3, other arithmetic, shards(): moved = jnp.sum(change * change)  12.1 us

commit v1 on v0

--- a/solution.py
+++ b/solution.py
@@ -5,6 +5,15 @@
 from jax.sharding import PartitionSpec as P
 
 ITERS = 4
+
+
+def sum_by_hops(shard, axis):
+    size = lax.axis_size(axis)
+    result, hop = (shard, 1)
+    while hop < size:
+        result = result + lax.ppermute(result, axis, [(i, i ^ hop) for i in range(size)])
+        hop = 2 * hop
+    return result
 
 
 def shards(cost, plan, row_mass, col_mass, row_dual, col_dual):
@@ -27,7 +36,7 @@
         new_row = row_dual + dual_step * (row_mass - row_total)
         row_square = jnp.sum((new_row - row_dual) ** 2)
         col_local = jnp.sum(extrap, axis=0)
-        col_total = lax.psum(col_local, "wide")
+        col_total = sum_by_hops(col_local, "wide")
         new_col = col_dual + dual_step * (col_mass - col_total)
         col_share = jnp.sum((new_col - col_dual) ** 2) / wide_count
         dual_share = row_square / narrow_count + col_share

time: 315 us -> 211 us (0.67)
  blocking collectives: 284 us -> 145 us
  starting transfers between devices: 0 us -> 23.2 us
  waiting for transfers between devices: 0 us -> 11.4 us
    psum x4 -> x0, blocking collectives: 147 us -> none  [shards(): col_total = lax.psum(col_local, 'wide')]
    ppermute x0 -> x12, starting transfers between devices: none -> 23.2 us  [sum_by_hops(): lax.ppermute(result, axis, [(i, i ^ hop) for i in range(size)])]
    ppermute x0 -> x12, waiting for transfers between devices: none -> 11.4 us  [sum_by_hops(): lax.ppermute(result, axis, [(i, i ^ hop) for i in range(size)])]
    psum x3, blocking collectives: 112 us -> 122 us  [shards(): dual_moved = lax.psum(dual_share, ('wide', 'narrow'))]
  transfers between devices with their start and end apart: 0 -> 12, of which waited for: 0 -> 8; matrix products, arithmetic and copies ran while one was open for 0% -> 1% of each run, Pallas kernels for 0% -> 0%
where the time goes in v1:
time: 211 us
  blocking collectives  145 us (69%)
  starting transfers between devices  23.2 us (11%)
  other arithmetic  21.8 us (10%)
  waiting for transfers between devices  11.4 us (5%)
  between operations  9.03 us (4%)
    psum x3, blocking collectives, shards(): dual_moved = lax.psum(dual_share, ('wide', 'narrow'))  122 us
    ppermute x12, starting transfers between devices, sum_by_hops(): lax.ppermute(result, axis, [(i, i ^ hop) for i in range(size)])  23.2 us
    psum x4, blocking collectives, shards(): row_total = lax.psum(jnp.sum(extrap, axis=1), 'narrow')  22.8 us
    reduce_sum x3, other arithmetic, shards(): moved = jnp.sum(change * change)  12.1 us
    ppermute x12, waiting for transfers between devices, sum_by_hops(): lax.ppermute(result, axis, [(i, i ^ hop) for i in range(size)])  11.4 us
    reduce_sum x1, other arithmetic, shards(): col_local = jnp.sum(extrap, axis=0)  4.91 us
  transfers between devices with their start and end apart: 12, of which 8 were waited for; matrix products, arithmetic and copies ran while one was open for 1% of the time, Pallas kernels for 0%

profile of v1, /device:TPU:0, one launch (start us, length us, event | category | flops | bytes accessed | tf_op | source)
XLA Modules:
  0.0 210.6 jit_solution(1587586112322570426)
XLA Ops:
  0.6 0.0 copy-start.1
  0.6 0.0 copy-start.3
  0.7 0.0 copy-start
  0.7 0.0 copy-start.4
  0.7 0.0 copy-start.2
  0.7 4.2 %multiply_reduce_fusion.2 = (f32[]{:T(128)}, f32[4096]{0:T(1024)S(1)}, f32[128]{0:T(128)S(1)}) fusion(f32[128,4096]{1,0:T(8,128)} %param.7, f32[4096]{0:T(1024)} %param.11, f32[128,4096]{1,0:T(8,128)} %param.6, f32[128]{0:T(128)} %param.10), kind=kLoop, calls=%fused_computation.6 | loop fusion | flops 5238655 | bytes 4228100 | tf_op jit(solution)/shard_map/reduce_sum | solution.py:34
  4.8 3.0 %collective-permute-start = (f32[4096]{0:T(1024)S(1)}, f32[4096]{0:T(1024)S(1)}, u32[]{:S(2)}, u32[]{:S(2)}) collective-permute-start(f32[4096]{0:T(1024)S(1)} %get-tuple-element.12), channel_id=1, source_target_pairs={{0,4},{4,0},{8,12},{12,8},{16,20},{20,16},{24,28},{28,24},{1,5},{5... | collective-permute-start | bytes 49160 | tf_op jit(solution)/shard_map/ppermute | solution.py:14
  7.8 1.7 collective-permute-done
  9.5 2.1 %collective-permute-start.1 = (f32[4096]{0:T(1024)S(1)}, f32[4096]{0:T(1024)S(1)}, u32[]{:S(2)}, u32[]{:S(2)}) collective-permute-start(f32[4096]{0:T(1024)S(1)} %add.121), channel_id=1, source_target_pairs={{0,8},{4,12},{8,0},{12,4},{16,24},{20,28},{24,16},{28,20},{1,9},{5... | collective-permute-start | bytes 49160 | tf_op jit(solution)/shard_map/ppermute | solution.py:14
  11.6 5.6 %psum.70 = f32[128]{0:T(128)S(1)} all-reduce(f32[128]{0:T(128)S(1)} %get-tuple-element.13), channel_id=1, replica_groups=mesh['wide'=8,'narrow'=4] {'narrow'}, use_global_device_ids=true, to_apply=%region_1.0 | all-reduce | flops 128 | bytes 1024 | tf_op jit(solution)/shard_map/psum | solution.py:35
  17.3 0.0 collective-permute-done.1
  17.3 2.7 %collective-permute-start.2 = (f32[4096]{0:T(1024)S(1)}, f32[4096]{0:T(1024)S(1)}, u32[]{:S(2)}, u32[]{:S(2)}) collective-permute-start(f32[4096]{0:T(1024)S(1)} %add.122), channel_id=1, source_target_pairs={{0,16},{4,20},{8,24},{12,28},{16,0},{20,4},{24,8},{28,12},{1,17},{... | collective-permute-start | bytes 49160 | tf_op jit(solution)/shard_map/ppermute | solution.py:14
  19.9 0.0 copy-done.3
  19.9 0.0 copy-done.4
  19.9 0.6 multiply_reduce_fusion.8
  21.2 0.8 collective-permute-done.2
  22.0 0.0 copy-done.1
  22.0 0.0 copy-done.2
  22.0 0.6 multiply_reduce_fusion.5
  23.3 40.9 %all-reduce.2 = (f32[]{:T(128)}, f32[]{:T(128)}) all-reduce(f32[]{:T(128)S(6)} %add.125, f32[]{:T(128)} %get-tuple-element.11), channel_id=1, replica_groups=mesh['wide'=8,'narrow'=4] {'wide','narrow'}, use_global_device_ids=true, to_apply=%region_5.0 | all-reduce | flops 2 | bytes 16 | tf_op jit(solution)/shard_map/psum | solution.py:44
  65.6 0.0 copy-done
  65.6 3.7 %multiply_reduce_fusion.1 = (f32[]{:T(128)}, f32[128]{0:T(128)S(1)}, f32[4096]{0:T(1024)S(1)}) fusion(f32[4096]{0:T(1024)S(1)} %get-tuple-element.30, f32[128,4096]{1,0:T(8,128)} %param.6, f32[128]{0:T(128)S(1)} %get-tuple-element.32, f32[]{:T(128)S(6)} %div.39, f32[128,4096]{1,0:T(8,128)S(1)} %copy-done, f32[4096]{0:T(1024)S(1)} %copy-done.1, ...), kind=kLoop, calls=%fused_computation.4 | loop fusion | flops 7860095 | bytes 4245000 | tf_op jit(solution)/shard_map/reduce_sum | solution.py:34
  69.3 2.3 %collective-permute-start.3 = (f32[4096]{0:T(1024)S(1)}, f32[4096]{0:T(1024)S(1)}, u32[]{:S(2)}, u32[]{:S(2)}) collective-permute-start(f32[4096]{0:T(1024)S(1)} %get-tuple-element.10), channel_id=1, source_target_pairs={{0,4},{4,0},{8,12},{12,8},{16,20},{20,16},{24,28},{28,24},{1,5},{5... | collective-permute-start | bytes 49160 | tf_op jit(solution)/shard_map/ppermute | solution.py:14
  71.6 1.7 collective-permute-done.3
  73.3 0.5 collective-permute-start.4
  73.8 5.7 %psum.73 = f32[128]{0:T(128)S(1)} all-reduce(f32[128]{0:T(128)S(1)} %get-tuple-element.9), channel_id=1, replica_groups=mesh['wide'=8,'narrow'=4] {'narrow'}, use_global_device_ids=true, to_apply=%region_9.0 | all-reduce | flops 128 | bytes 1024 | tf_op jit(solution)/shard_map/psum | solution.py:35
  79.5 0.0 collective-permute-done.4
  79.5 2.5 %collective-permute-start.5 = (f32[4096]{0:T(1024)S(1)}, f32[4096]{0:T(1024)S(1)}, u32[]{:S(2)}, u32[]{:S(2)}) collective-permute-start(f32[4096]{0:T(1024)S(1)} %add.131), channel_id=1, source_target_pairs={{0,16},{4,20},{8,24},{12,28},{16,0},{20,4},{24,8},{28,12},{1,17},{... | collective-permute-start | bytes 49160 | tf_op jit(solution)/shard_map/ppermute | solution.py:14
  82.0 0.6 multiply_reduce_fusion.7
  83.2 1.0 collective-permute-done.5
  84.2 0.6 multiply_reduce_fusion.4
  85.5 40.3 %all-reduce.1 = (f32[]{:T(128)}, f32[]{:T(128)}) all-reduce(f32[]{:T(128)S(6)} %add.134, f32[]{:T(128)} %get-tuple-element.8), channel_id=1, replica_groups=mesh['wide'=8,'narrow'=4] {'wide','narrow'}, use_global_device_ids=true, to_apply=%region_13.0 | all-reduce | flops 2 | bytes 16 | tf_op jit(solution)/shard_map/psum | solution.py:44
  127.3 4.2 %multiply_reduce_fusion = (f32[]{:T(128)}, f32[128]{0:T(128)S(1)}, f32[4096]{0:T(1024)S(1)}) fusion(f32[4096]{0:T(1024)S(1)} %get-tuple-element.26, f32[128,4096]{1,0:T(8,128)} %param.6, f32[128]{0:T(128)S(1)} %get-tuple-element.28, f32[]{:T(128)S(6)} %div.43, f32[4096]{0:T(1024)S(1)} %get-tuple-element.30, f32[128]{0:T(128)S(1)} %get-tuple-element.32, ...), kind=kLoop, calls=%fused_computation.2 | loop fusion | flops 10481535 | bytes 4261900 | tf_op jit(solution)/shard_map/reduce_sum | solution.py:34
  131.4 2.3 %collective-permute-start.6 = (f32[4096]{0:T(1024)S(1)}, f32[4096]{0:T(1024)S(1)}, u32[]{:S(2)}, u32[]{:S(2)}) collective-permute-start(f32[4096]{0:T(1024)S(1)} %get-tuple-element.7), channel_id=1, source_target_pairs={{0,4},{4,0},{8,12},{12,8},{16,20},{20,16},{24,28},{28,24},{1,5},{5... | collective-permute-start | bytes 49160 | tf_op jit(solution)/shard_map/ppermute | solution.py:14
  133.7 1.7 collective-permute-done.6
  135.4 0.4 collective-permute-start.7
  135.9 5.7 %psum.76 = f32[128]{0:T(128)S(1)} all-reduce(f32[128]{0:T(128)S(1)} %get-tuple-element.6), channel_id=1, replica_groups=mesh['wide'=8,'narrow'=4] {'narrow'}, use_global_device_ids=true, to_apply=%region_17.0 | all-reduce | flops 128 | bytes 1024 | tf_op jit(solution)/shard_map/psum | solution.py:35
  141.6 0.0 collective-permute-done.7
  141.6 2.4 %collective-permute-start.8 = (f32[4096]{0:T(1024)S(1)}, f32[4096]{0:T(1024)S(1)}, u32[]{:S(2)}, u32[]{:S(2)}) collective-permute-start(f32[4096]{0:T(1024)S(1)} %add.140), channel_id=1, source_target_pairs={{0,16},{4,20},{8,24},{12,28},{16,0},{20,4},{24,8},{28,12},{1,17},{... | collective-permute-start | bytes 49160 | tf_op jit(solution)/shard_map/ppermute | solution.py:14
  144.0 0.6 multiply_reduce_fusion.6
  145.3 1.1 collective-permute-done.8
  146.3 0.6 multiply_reduce_fusion.3
  147.6 41.2 %all-reduce = (f32[]{:T(128)}, f32[]{:T(128)}) all-reduce(f32[]{:T(128)S(6)} %add.143, f32[]{:T(128)} %get-tuple-element.5), channel_id=1, replica_groups=mesh['wide'=8,'narrow'=4] {'wide','narrow'}, use_global_device_ids=true, to_apply=%region_21.0 | all-reduce | flops 2 | bytes 16 | tf_op jit(solution)/shard_map/psum | solution.py:44
  190.2 4.9 %fusion.6 = (f32[4096]{0:T(1024)S(1)}, f32[128]{0:T(128)S(1)}, f32[128,4096]{1,0:T(8,128)}) fusion(f32[4096]{0:T(1024)S(1)} %get-tuple-element.26, f32[128,4096]{1,0:T(8,128)} %param.6, f32[128]{0:T(128)S(1)} %get-tuple-element.28, f32[]{:T(128)S(6)} %div.43, f32[4096]{0:T(1024)S(1)} %get-tuple-element.30, f32[128]{0:T(128)S(1)} %get-tuple-element.32, ...), kind=kLoop, calls=%fused_computation.17 | loop fusion | flops 12054400 | bytes 6375948 | tf_op jit(solution)/shard_map/reduce_sum | solution.py:38
  195.1 2.3 %collective-permute-start.9 = (f32[4096]{0:T(1024)S(1)}, f32[4096]{0:T(1024)S(1)}, u32[]{:S(2)}, u32[]{:S(2)}) collective-permute-start(f32[4096]{0:T(1024)S(1)} %get-tuple-element.3), channel_id=1, source_target_pairs={{0,4},{4,0},{8,12},{12,8},{16,20},{20,16},{24,28},{28,24},{1,5},{5... | collective-permute-start | bytes 49160 | tf_op jit(solution)/shard_map/ppermute | solution.py:14
  197.4 1.7 collective-permute-done.9
  199.1 0.4 collective-permute-start.10
  199.5 5.7 %psum.79 = f32[128]{0:T(128)S(1)} all-reduce(f32[128]{0:T(128)S(1)} %get-tuple-element.4), channel_id=1, replica_groups=mesh['wide'=8,'narrow'=4] {'narrow'}, use_global_device_ids=true, to_apply=%region_25.0 | all-reduce | flops 128 | bytes 1024 | tf_op jit(solution)/shard_map/psum | solution.py:35
  205.3 0.0 collective-permute-done.10
  205.3 2.5 %collective-permute-start.11 = (f32[4096]{0:T(1024)S(1)}, f32[4096]{0:T(1024)S(1)}, u32[]{:S(2)}, u32[]{:S(2)}) collective-permute-start(f32[4096]{0:T(1024)S(1)} %add.149), channel_id=1, source_target_pairs={{0,16},{4,20},{8,24},{12,28},{16,0},{20,4},{24,8},{28,12},{1,17},{... | collective-permute-start | bytes 49160 | tf_op jit(solution)/shard_map/ppermute | solution.py:14
  207.8 0.5 multiply_add_fusion.4
  208.3 1.7 collective-permute-done.11
  210.0 0.6 multiply_add_fusion
  (8 shorter events, 0.0 us)
Async XLA Ops:
  0.6 21.4 %copy-start.1 = (f32[4096]{0:T(1024)S(1)}, f32[4096]{0:T(1024)}, u32[]{:S(2)}) copy-start(f32[4096]{0:T(1024)} %param.11) | copy-start | bytes 49156
  0.6 19.3 %copy-start.3 = (f32[128]{0:T(128)S(1)}, f32[128]{0:T(128)}, u32[]{:S(2)}) copy-start(f32[128]{0:T(128)} %param.10) | copy-start | bytes 1540
  0.7 65.0 %copy-start = (f32[128,4096]{1,0:T(8,128)S(1)}, f32[128,4096]{1,0:T(8,128)}, u32[]{:S(2)}) copy-start(f32[128,4096]{1,0:T(8,128)} %param.7) | copy-start | bytes 6291460
  0.7 19.3 %copy-start.4 = (f32[128]{0:T(128)S(1)}, f32[128]{0:T(128)}, u32[]{:S(2)}) copy-start(f32[128]{0:T(128)} %param.8) | copy-start | bytes 1540
  0.7 21.3 %copy-start.2 = (f32[4096]{0:T(1024)S(1)}, f32[4096]{0:T(1024)}, u32[]{:S(2)}) copy-start(f32[4096]{0:T(1024)} %param.9) | copy-start | bytes 49156
  4.8 4.7 %collective-permute-start = (f32[4096]{0:T(1024)S(1)}, f32[4096]{0:T(1024)S(1)}, u32[]{:S(2)}, u32[]{:S(2)}) collective-permute-start(f32[4096]{0:T(1024)S(1)} %get-tuple-element.12), channel_id=1, source_target_pairs={{0,4},{4,0},{8,12},{12,8},{16,20},{20,16},{24,28},{28,24},{1,5},{5... | collective-permute-start | bytes 49160 | tf_op jit(solution)/shard_map/ppermute | solution.py:14
  9.5 7.7 %collective-permute-start.1 = (f32[4096]{0:T(1024)S(1)}, f32[4096]{0:T(1024)S(1)}, u32[]{:S(2)}, u32[]{:S(2)}) collective-permute-start(f32[4096]{0:T(1024)S(1)} %add.121), channel_id=1, source_target_pairs={{0,8},{4,12},{8,0},{12,4},{16,24},{20,28},{24,16},{28,20},{1,9},{5... | collective-permute-start | bytes 49160 | tf_op jit(solution)/shard_map/ppermute | solution.py:14
  17.3 4.7 %collective-permute-start.2 = (f32[4096]{0:T(1024)S(1)}, f32[4096]{0:T(1024)S(1)}, u32[]{:S(2)}, u32[]{:S(2)}) collective-permute-start(f32[4096]{0:T(1024)S(1)} %add.122), channel_id=1, source_target_pairs={{0,16},{4,20},{8,24},{12,28},{16,0},{20,4},{24,8},{28,12},{1,17},{... | collective-permute-start | bytes 49160 | tf_op jit(solution)/shard_map/ppermute | solution.py:14
  69.3 4.0 %collective-permute-start.3 = (f32[4096]{0:T(1024)S(1)}, f32[4096]{0:T(1024)S(1)}, u32[]{:S(2)}, u32[]{:S(2)}) collective-permute-start(f32[4096]{0:T(1024)S(1)} %get-tuple-element.10), channel_id=1, source_target_pairs={{0,4},{4,0},{8,12},{12,8},{16,20},{20,16},{24,28},{28,24},{1,5},{5... | collective-permute-start | bytes 49160 | tf_op jit(solution)/shard_map/ppermute | solution.py:14
  73.3 6.2 %collective-permute-start.4 = (f32[4096]{0:T(1024)S(1)}, f32[4096]{0:T(1024)S(1)}, u32[]{:S(2)}, u32[]{:S(2)}) collective-permute-start(f32[4096]{0:T(1024)S(1)} %add.130), channel_id=1, source_target_pairs={{0,8},{4,12},{8,0},{12,4},{16,24},{20,28},{24,16},{28,20},{1,9},{5... | collective-permute-start | bytes 49160 | tf_op jit(solution)/shard_map/ppermute | solution.py:14
  79.5 4.7 %collective-permute-start.5 = (f32[4096]{0:T(1024)S(1)}, f32[4096]{0:T(1024)S(1)}, u32[]{:S(2)}, u32[]{:S(2)}) collective-permute-start(f32[4096]{0:T(1024)S(1)} %add.131), channel_id=1, source_target_pairs={{0,16},{4,20},{8,24},{12,28},{16,0},{20,4},{24,8},{28,12},{1,17},{... | collective-permute-start | bytes 49160 | tf_op jit(solution)/shard_map/ppermute | solution.py:14
  131.4 4.0 %collective-permute-start.6 = (f32[4096]{0:T(1024)S(1)}, f32[4096]{0:T(1024)S(1)}, u32[]{:S(2)}, u32[]{:S(2)}) collective-permute-start(f32[4096]{0:T(1024)S(1)} %get-tuple-element.7), channel_id=1, source_target_pairs={{0,4},{4,0},{8,12},{12,8},{16,20},{20,16},{24,28},{28,24},{1,5},{5... | collective-permute-start | bytes 49160 | tf_op jit(solution)/shard_map/ppermute | solution.py:14
  135.4 6.2 %collective-permute-start.7 = (f32[4096]{0:T(1024)S(1)}, f32[4096]{0:T(1024)S(1)}, u32[]{:S(2)}, u32[]{:S(2)}) collective-permute-start(f32[4096]{0:T(1024)S(1)} %add.139), channel_id=1, source_target_pairs={{0,8},{4,12},{8,0},{12,4},{16,24},{20,28},{24,16},{28,20},{1,9},{5... | collective-permute-start | bytes 49160 | tf_op jit(solution)/shard_map/ppermute | solution.py:14
  141.6 4.7 %collective-permute-start.8 = (f32[4096]{0:T(1024)S(1)}, f32[4096]{0:T(1024)S(1)}, u32[]{:S(2)}, u32[]{:S(2)}) collective-permute-start(f32[4096]{0:T(1024)S(1)} %add.140), channel_id=1, source_target_pairs={{0,16},{4,20},{8,24},{12,28},{16,0},{20,4},{24,8},{28,12},{1,17},{... | collective-permute-start | bytes 49160 | tf_op jit(solution)/shard_map/ppermute | solution.py:14
  195.1 4.0 %collective-permute-start.9 = (f32[4096]{0:T(1024)S(1)}, f32[4096]{0:T(1024)S(1)}, u32[]{:S(2)}, u32[]{:S(2)}) collective-permute-start(f32[4096]{0:T(1024)S(1)} %get-tuple-element.3), channel_id=1, source_target_pairs={{0,4},{4,0},{8,12},{12,8},{16,20},{20,16},{24,28},{28,24},{1,5},{5... | collective-permute-start | bytes 49160 | tf_op jit(solution)/shard_map/ppermute | solution.py:14
  199.1 6.2 %collective-permute-start.10 = (f32[4096]{0:T(1024)S(1)}, f32[4096]{0:T(1024)S(1)}, u32[]{:S(2)}, u32[]{:S(2)}) collective-permute-start(f32[4096]{0:T(1024)S(1)} %add.148), channel_id=1, source_target_pairs={{0,8},{4,12},{8,0},{12,4},{16,24},{20,28},{24,16},{28,20},{1,9},{5... | collective-permute-start | bytes 49160 | tf_op jit(solution)/shard_map/ppermute | solution.py:14
  205.3 4.7 %collective-permute-start.11 = (f32[4096]{0:T(1024)S(1)}, f32[4096]{0:T(1024)S(1)}, u32[]{:S(2)}, u32[]{:S(2)}) collective-permute-start(f32[4096]{0:T(1024)S(1)} %add.149), channel_id=1, source_target_pairs={{0,16},{4,20},{8,24},{12,28},{16,0},{20,4},{24,8},{28,12},{1,17},{... | collective-permute-start | bytes 49160 | tf_op jit(solution)/shard_map/ppermute | solution.py:14
